TPU v7x, 32 devices: a whole 2x2x4 slice. The times are simulated.
32 devices in a mesh: groups: 2 (over x), mesh: 16 (over z, y, core).
Axes of the slice: x: 2, y: 2, z: 4, core: 2. Of those that a mesh axis runs over, the one named last changes fastest.
Arguments:
- state: float32 [3, 64, 32768], P(None, None, ('groups', 'mesh')), parts along dimension 2, may hold values from -6 to 6
- depth: float32 [32768], P(('groups', 'mesh')), parts along dimension 0, may hold values from 0.5 to 4
- coef: float32 [2, 6, 32768], P(None, None, ('groups', 'mesh')), parts along dimension 2, may hold values from -2 to 2
- wet_faces: int32 [6, 32768], P(None, ('groups', 'mesh')), parts along dimension 1, may hold values 0 or 1
- conn: int32 [6, 32768], P(None, ('groups', 'mesh')), parts along dimension 1, may hold values from 0 to 1535, as said below
- send_list: int32 [2, 8192], P(None, ('groups', 'mesh')), parts along dimension 1, may hold values from 0 to 1023, as said below
- obs_nodes: int32 [3, 32768], P(None, ('groups', 'mesh')), parts along dimension 1, may hold values from 0 to 1023
- obs_weight: float32 [3, 32768], P(None, ('groups', 'mesh')), parts along dimension 1, may hold values from 0 to 1, as said below
- obs_value: float32 [32768], P(('groups', 'mesh')), parts along dimension 0, may hold values from -9 to 9
- obs_error: float32 [32768], P(('groups', 'mesh')), parts along dimension 0, may hold values from 0.5 to 2
- loc_ids: int32 [32, 512], P(('groups', 'mesh')), parts along dimension 0, may hold values from 0 to 16383, as said below
- loc_len: int32 [32], P(('groups', 'mesh')), parts along dimension 0, may hold values from 64 to 512, as said below
- loc_weight: float32 [32, 512], P(('groups', 'mesh')), parts along dimension 0, may hold values from 0.05 to 1
Outputs:
- analysis: float32 [3, 64, 32768], P(None, None, ('groups', 'mesh')), parts along dimension 2
There are 2 independent parts, one for each index of `groups`. A program takes and returns all parts, laid end to end along the dimension named above; each array names one. Nothing has to cross between parts.
Inputs may be any that keep to these rules, and one draw needn't show every extreme that they name: `conn`: for each partition: below 1024 a local node; 1024 + p is slot p of the lower partition's list toward it, 1280 + p slot p of the higher partition's list toward it; the first partition names no lower slot and the last no higher one. `send_list`: each partition's two lists hold 256 distinct local node numbers each. `obs_weight`: the three weights of an observation are positive and sum to one. `loc_ids`: the entries of a patch's list are distinct and name observations held by the patch's partition or the two beside it. `loc_len`: patch 0 has a list of length 512.
All inputs are finite; a program needn't handle non-finite values. No bound on the sum of `wet_faces` on one device may be relied on, other than what follows from the above.
Results may differ from a plain program's by a relative error of at most 0.0003.
Values sent between devices are 32-bit elements; how exact they have to be, the bound alone decides.
A program may use at most 64 MiB of HBM per device.

v0:
```python
import functools
import math

import jax
import jax.numpy as jnp
from jax import lax
from jax.experimental import pallas as pl
from jax.experimental.pallas import tpu as pltpu
from jax.sharding import PartitionSpec as P

STEPS = 2
DT = 0.1
TOPMOST = lax.Precision.HIGHEST
LANES = 128
CHUNK = 256
F32, BF16 = jnp.float32, jnp.bfloat16


def halves(x):
    high = x.astype(BF16)
    return high, (x - high.astype(F32)).astype(BF16)


def dot(a, b):
    return jnp.dot(a, b, preferred_element_type=F32)


def merge_slots(ids, weights):
    ids, weights = list(ids), [list(w) for w in weights]
    for s in range(1, len(ids)):
        for t in range(s):
            same = ids[s] == ids[t]
            for w in weights:
                w[t] = w[t] + jnp.where(same, w[s], 0.0)
            ids[s] = jnp.where(same, -1, ids[s])
    return ids, weights


def build(out_ref, places, extent, ids_ref, parts_ref, slots, kinds):
    columns = ids_ref.shape[1]
    rows = 16

    def column(c, _):
        cols = pl.ds(pl.multiple_of(c * LANES, LANES), LANES)
        ids = [jnp.broadcast_to(ids_ref[s : s + 1, cols], (rows, LANES)).astype(jnp.int16) for s in range(slots)]
        parts = [
            [jnp.broadcast_to(parts_ref[q * slots + s : q * slots + s + 1, cols], (rows, LANES)).astype(BF16) for s in range(slots)]
            for q in range(kinds)
        ]
        blank = jnp.zeros((rows, LANES), BF16)

        unroll = 4

        def block(r, _):
            for u in range(unroll):
                start = pl.multiple_of((r * unroll + u) * rows, rows)
                here = places + jnp.full((rows, LANES), start, jnp.int32).astype(jnp.int16)
                total = [blank] * kinds
                for s in range(slots):
                    hit = here == ids[s]
                    total = [jnp.where(hit, parts[q][s], total[q]) for q in range(kinds)]
                for q in range(kinds):
                    out_ref[q, pl.ds(start, rows), cols] = total[q]
            return 0

        lax.fori_loop(0, extent // (rows * unroll), block, 0)
        return 0

    lax.fori_loop(0, columns // LANES, column, 0)


def linv_of(table, unit, members):
    width = 8
    work = jnp.concatenate([table, unit], axis=1)
    count = members // width
    blocks = [work[b * width : (b + 1) * width] for b in range(count)]
    done = []
    for b in range(count):
        first = b * width
        panel = blocks[b]
        rows = [panel[j : j + 1] for j in range(width)]
        below = blocks[b + 1 :]
        cols = [[blk[:, first + j : first + j + 1] for blk in below] for j in range(width)]
        corner = [[panel[j : j + 1, first + i : first + i + 1] for i in range(width)] for j in range(width)]
        scaled = []
        for j in range(width):
            inverse = 1.0 / corner[j][j]
            unit_row = rows[j] * inverse
            scaled.append(unit_row)
            for i in range(j + 1, width):
                factor = corner[j][i]
                rows[i] = rows[i] - factor * unit_row
                scale = factor * inverse
                cols[i] = [ci - cj * scale for ci, cj in zip(cols[i], cols[j])]
                for k in range(i, width):
                    value = corner[i][k] - scale * corner[j][k]
                    corner[i][k] = value
                    corner[k][i] = value
        for j in range(width):
            done.append(rows[j] * lax.rsqrt(corner[j][j]))
        for n in range(len(below)):
            total = below[n]
            for j in range(width):
                total = total - cols[j][n] * scaled[j]
            blocks[b + 1 + n] = total
    return jnp.concatenate(done, axis=0)[:, members:]


def kernel(
    n, state, depth, coef, wet, conn, lists, obs_nodes, obs_weight, obs_value, obs_error, loc_ids, loc_len, loc_weight,
    out, field, operator, picker, sampler, slot_ids, slot_parts, obs_ids, obs_parts, totals, mixed, gather_mixed,
    sums, send_flow, got_flow, send_level, got_level, shares, got_shares, grams, got_grams, anomalies, send_sem, recv_sem,
):
    me = lax.axis_index("mesh")
    lower, upper = lax.rem(me + n - 1, n), lax.rem(me + 1, n)
    has_lower, has_upper = me > 0, me < n - 1
    members, nodes = state.shape[1], state.shape[2]
    slots, corners = conn.shape[0], obs_nodes.shape[0]
    width = lists.shape[1]
    extent = nodes + 2 * width
    obs_count = obs_value.shape[1]

    barrier = pltpu.get_barrier_semaphore()

    @pl.when(has_lower)
    def _():
        pl.semaphore_signal(barrier, inc=1, device_id={"mesh": lower}, device_id_type=pl.DeviceIdType.MESH)

    @pl.when(has_upper)
    def _():
        pl.semaphore_signal(barrier, inc=1, device_id={"mesh": upper}, device_id_type=pl.DeviceIdType.MESH)

    def pair(k, source, target):
        down = pltpu.make_async_remote_copy(
            src_ref=source.at[0], dst_ref=target.at[1], send_sem=send_sem.at[k, 0], recv_sem=recv_sem.at[k, 0],
            device_id={"mesh": lower}, device_id_type=pl.DeviceIdType.MESH,
        )
        up = pltpu.make_async_remote_copy(
            src_ref=source.at[1], dst_ref=target.at[0], send_sem=send_sem.at[k, 1], recv_sem=recv_sem.at[k, 1],
            device_id={"mesh": upper}, device_id_type=pl.DeviceIdType.MESH,
        )
        return down, up

    def start(copies):
        pl.when(has_lower)(copies[0].start)
        pl.when(has_upper)(copies[1].start)

    def arrive(copies):
        pl.when(has_upper)(copies[0].wait_recv)
        pl.when(has_lower)(copies[1].wait_recv)

    def sent(copies):
        pl.when(has_lower)(copies[0].wait_send)
        pl.when(has_upper)(copies[1].wait_send)

    flow_copies = [pair(i, send_flow.at[i], got_flow.at[i]) for i in range(STEPS)]
    level_copies = [pair(STEPS + i, send_level.at[i], got_level.at[i]) for i in range(STEPS)]
    share_copies = pair(2 * STEPS, shares, got_shares)
    gram_copies = pair(2 * STEPS + 1, grams, got_grams)

    def blank_side(side):
        for i in range(STEPS):
            got_flow[i, side] = jnp.zeros_like(got_flow[i, side])
            got_level[i, side] = jnp.zeros_like(got_level[i, side])
        got_shares[side] = jnp.zeros_like(got_shares[side])
        got_grams[side] = jnp.zeros_like(got_grams[side])

    pl.when(me == 0)(lambda: blank_side(0))
    pl.when(me == n - 1)(lambda: blank_side(1))

    places = lax.broadcasted_iota(jnp.int32, (16, LANES), 0).astype(jnp.int16)

    def pick_column(c, _):
        cols = pl.ds(pl.multiple_of(c * LANES, LANES), LANES)
        for h in range(2):
            ids = jnp.broadcast_to(lists[h : h + 1, cols], (16, LANES)).astype(jnp.int16)

            def block(r, _):
                begin = pl.multiple_of(r * 16, 16)
                here = places + jnp.full((16, LANES), begin, jnp.int32).astype(jnp.int16)
                picker[h, pl.ds(begin, 16), cols] = jnp.where(here == ids, jnp.ones((16, LANES), BF16), jnp.zeros((16, LANES), BF16))
                return 0

            lax.fori_loop(0, nodes // 16, block, 0, unroll=4)
        return 0

    lax.fori_loop(0, width // LANES, pick_column, 0)

    def split_field(f, values, cols):
        high, low = halves(values)
        mixed[2 * f * members : (2 * f + 1) * members, cols] = high
        mixed[(2 * f + 1) * members : (2 * f + 2) * members, cols] = low

    def send_fields(first, number, target):
        for h in range(2):
            picked = dot(mixed[2 * first * members : 2 * (first + number) * members, :], picker[h])
            for f in range(number):
                base = 2 * f * members
                target[h, f * members : (f + 1) * members, :] = (
                    picked[base : base + members] + picked[base + members : base + 2 * members]
                )

    def over_chunks(body):
        def step(c, _):
            body(pl.ds(pl.multiple_of(c * CHUNK, CHUNK), CHUNK))
            return 0

        lax.fori_loop(0, nodes // CHUNK, step, 0)

    def product(pairs_ref, base, op, rows, cols):
        both = dot(pairs_ref[base : base + 2 * members, :], operator[2 * op, rows, cols])
        cross = dot(pairs_ref[base : base + members, :], operator[2 * op + 1, rows, cols])
        return both[:members] + both[members:] + cross

    local_rows, ghost_rows = slice(0, nodes), slice(nodes, extent)

    def first_split(cols):
        for f in (1, 2):
            split_field(f, state[f, :, cols], cols)

    over_chunks(first_split)
    send_fields(1, 2, send_flow.at[0])

    pl.semaphore_wait(barrier, jnp.minimum(me, 1) + jnp.minimum(n - 1 - me, 1))
    start(flow_copies[0])

    list_size = loc_ids.shape[1]
    groups = 3 * obs_count // LANES
    live = lax.broadcasted_iota(jnp.int32, (1, list_size), 1) < loc_len[0]
    entry = jnp.where(live, loc_weight[...], 0.0)
    position = loc_ids[...] - (me - 1) * obs_count
    major, minor = position // LANES, lax.rem(position, LANES)
    coarse = jnp.where(lax.broadcasted_iota(jnp.int32, (groups, list_size), 0) == major, entry, 0.0)
    fine = jnp.where(lax.broadcasted_iota(jnp.int32, (LANES, list_size), 0) == minor, 1.0, 0.0)
    dense = lax.dot_general(coarse, fine, (((1,), (1,)), ((), ())), precision=TOPMOST, preferred_element_type=F32)
    third = groups // 3
    shares[0] = dense[:third]
    shares[1] = dense[2 * third :]
    own_share = dense[third : 2 * third]
    start(share_copies)

    faces = wet[...].astype(F32)
    east, north = faces * coef[0], faces * coef[1]
    totals[0:1] = jnp.sum(east, axis=0, keepdims=True)
    totals[1:2] = jnp.sum(north, axis=0, keepdims=True)
    ids, (east_slots, north_slots) = merge_slots(
        [conn[s : s + 1] for s in range(slots)],
        [[east[s : s + 1] for s in range(slots)], [north[s : s + 1] for s in range(slots)]],
    )
    for s in range(slots):
        slot_ids[s : s + 1] = ids[s]
        for q, w in enumerate((east_slots[s], north_slots[s])):
            high, low = halves(w)
            slot_parts[2 * q * slots + s : 2 * q * slots + s + 1] = high.astype(F32)
            slot_parts[(2 * q + 1) * slots + s : (2 * q + 1) * slots + s + 1] = low.astype(F32)
    build(operator, places, extent, slot_ids, slot_parts, slots, 4)

    ids, (weight_slots,) = merge_slots(
        [obs_nodes[s : s + 1] for s in range(corners)], [[obs_weight[s : s + 1] for s in range(corners)]]
    )
    for s in range(corners):
        obs_ids[s : s + 1] = ids[s]
        high, low = halves(weight_slots[s])
        obs_parts[s : s + 1] = high.astype(F32)
        obs_parts[corners + s : corners + s + 1] = low.astype(F32)

    for i in range(STEPS):
        old = state if i == 0 else field
        last = i == STEPS - 1

        def flow_local(cols, old=old):
            sums[0, :, cols] = (
                product(mixed, 2 * members, 0, local_rows, cols)
                + product(mixed, 4 * members, 1, local_rows, cols)
                - old[1, :, cols] * totals[0:1, cols]
                - old[2, :, cols] * totals[1:2, cols]
            )

        over_chunks(flow_local)
        if i == 0:
            build(sampler, places, nodes, obs_ids, obs_parts, corners, 2)
        arrive(flow_copies[i])
        for side in range(2):
            for f in range(2):
                high, low = halves(got_flow[i, side, f * members : (f + 1) * members, :])
                gather_mixed[2 * f * members : (2 * f + 1) * members, side * width : (side + 1) * width] = high
                gather_mixed[(2 * f + 1) * members : (2 * f + 2) * members, side * width : (side + 1) * width] = low

        def flow_ghost(cols, old=old):
            divergence = (
                sums[0, :, cols]
                + product(gather_mixed, 0, 0, ghost_rows, cols)
                + product(gather_mixed, 2 * members, 1, ghost_rows, cols)
            )
            level = old[0, :, cols] - DT * depth[0:1, cols] * divergence
            field[0, :, cols] = level
            split_field(0, level, cols)

        over_chunks(flow_ghost)
        send_fields(0, 1, send_level.at[i])
        start(level_copies[i])

        if last:
            arrive(share_copies)

            def observe(cols):
                both = dot(mixed[: 2 * members, :], sampler[0, :, cols])
                observed = both[:members] + both[members:] + dot(mixed[:members, :], sampler[1, :, cols])
                mean = jnp.mean(observed, axis=0, keepdims=True)
                anomalies[:members, cols] = observed - mean
                anomalies[members : members + 8, cols] = jnp.broadcast_to(obs_value[0:1, cols] - mean, (8, CHUNK))

            over_chunks(observe)
            precision = 1.0 / (obs_error[...] * obs_error[...])
            scaled = []
            for share in (got_shares[0], own_share, got_shares[1]):
                line = jnp.concatenate([share[a : a + 1] for a in range(third)], axis=1)
                scaled.append(anomalies[...] * (line * precision))
            table = lax.dot_general(
                jnp.concatenate(scaled, axis=0), anomalies[:members], (((1,), (1,)), ((), ())),
                precision=TOPMOST, preferred_element_type=F32,
            )
            tall = members + 8
            pad = jnp.zeros((tall, grams.shape[2] - members), F32)
            grams[0] = jnp.concatenate([table[:tall], pad], axis=1)
            grams[1] = jnp.concatenate([table[2 * tall :], pad], axis=1)
            own_table = table[tall : 2 * tall]
            start(gram_copies)

        def level_local(cols):
            level = field[0, :, cols]
            for d in range(2):
                sums[d, :, cols] = product(mixed, 0, d, local_rows, cols) - level * totals[d : d + 1, cols]

        over_chunks(level_local)
        arrive(level_copies[i])
        for side in range(2):
            high, low = halves(got_level[i, side])
            gather_mixed[:members, side * width : (side + 1) * width] = high
            gather_mixed[members : 2 * members, side * width : (side + 1) * width] = low

        def level_ghost(cols, old=old, last=last):
            for d in range(2):
                slope = sums[d, :, cols] + product(gather_mixed, 0, d, ghost_rows, cols)
                value = old[1 + d, :, cols] - DT * slope
                field[1 + d, :, cols] = value
                if not last:
                    split_field(1 + d, value, cols)

        over_chunks(level_ghost)
        if not last:
            send_fields(1, 2, send_flow.at[i + 1])
            start(flow_copies[i + 1])

    arrive(gram_copies)
    combined = own_table + got_grams[0, :, :members] + got_grams[1, :, :members]
    unit = jnp.where(
        lax.broadcasted_iota(jnp.int32, (members, members), 0) == lax.broadcasted_iota(jnp.int32, (members, members), 1), 1.0, 0.0
    )
    linv = linv_of(combined[:members] + (members - 1.0) * unit, unit, members)
    rhs = combined[members : members + 1]
    halfway = jnp.sum(linv * rhs, axis=1, keepdims=True)
    mean_w = jnp.sum(linv * halfway, axis=0, keepdims=True)
    blend = mean_w + math.sqrt(members - 1.0) * linv

    def analyse(cols):
        for c in range(3):
            forecast = field[c, :, cols]
            average = jnp.mean(forecast, axis=0, keepdims=True)
            out[c, :, cols] = average + jnp.dot(blend, forecast - average, precision=TOPMOST, preferred_element_type=F32)

    over_chunks(analyse)
    for copies in flow_copies + level_copies + [share_copies, gram_copies]:
        sent(copies)


def local(
    n, state, depth, coef, wet_faces, conn, send_list, obs_nodes, obs_weight, obs_value, obs_error, loc_ids, loc_len, loc_weight
):
    members, nodes = state.shape[1], state.shape[2]
    slots, corners, width = conn.shape[0], obs_nodes.shape[0], send_list.shape[1]
    obs_count = obs_value.shape[0]
    extent = nodes + 2 * width
    assert loc_ids.shape[0] == 1
    vmem = pl.BlockSpec(memory_space=pltpu.VMEM)
    smem = pl.BlockSpec(memory_space=pltpu.SMEM)
    number = 2 * STEPS + 2
    return pl.pallas_call(
        functools.partial(kernel, n),
        out_shape=jax.ShapeDtypeStruct(state.shape, F32),
        in_specs=[vmem] * 11 + [smem, vmem],
        out_specs=vmem,
        scratch_shapes=[
            pltpu.VMEM((3, members, nodes), F32),
            pltpu.VMEM((4, extent, nodes), BF16),
            pltpu.VMEM((2, nodes, width), BF16),
            pltpu.VMEM((2, nodes, obs_count), BF16),
            pltpu.VMEM((8, nodes), jnp.int32),
            pltpu.VMEM((4 * slots, nodes), F32),
            pltpu.VMEM((8, obs_count), jnp.int32),
            pltpu.VMEM((8, obs_count), F32),
            pltpu.VMEM((8, nodes), F32),
            pltpu.VMEM((6 * members, nodes), BF16),
            pltpu.VMEM((4 * members, 2 * width), BF16),
            pltpu.VMEM((2, members, nodes), F32),
            pltpu.VMEM((STEPS, 2, 2 * members, width), F32),
            pltpu.VMEM((STEPS, 2, 2 * members, width), F32),
            pltpu.VMEM((STEPS, 2, members, width), F32),
            pltpu.VMEM((STEPS, 2, members, width), F32),
            pltpu.VMEM((2, obs_count // LANES, LANES), F32),
            pltpu.VMEM((2, obs_count // LANES, LANES), F32),
            pltpu.VMEM((2, members + 8, LANES), F32),
            pltpu.VMEM((2, members + 8, LANES), F32),
            pltpu.VMEM((members + 8, obs_count), F32),
            pltpu.SemaphoreType.DMA((number, 2)),
            pltpu.SemaphoreType.DMA((number, 2)),
        ],
        compiler_params=pltpu.CompilerParams(collective_id=0, has_side_effects=True, vmem_limit_bytes=56 * 1024 * 1024),
    )(
        state, depth[None], coef, wet_faces, conn, send_list, obs_nodes, obs_weight, obs_value[None], obs_error[None],
        loc_ids, loc_len, loc_weight,
    )


def solution(mesh):
    split = ("groups", "mesh")
    in_specs = (
        P(None, None, split), P(split), P(None, None, split), P(None, split), P(None, split), P(None, split),
        P(None, split), P(None, split), P(split), P(split), P(split, None), P(split), P(split, None),
    )
    return jax.shard_map(
        functools.partial(local, mesh.shape["mesh"]), mesh=mesh, in_specs=in_specs, out_specs=P(None, None, split), check_vma=False
    )
```

profile of v0, /device:TPU:1, one launch (start us, length us, event | category | flops | bytes accessed | tf_op | source)
XLA Modules:
  0.0 48.7 jit_solution(10017557768581613758)
XLA Ops:
  0.7 1.4 %copy.14.coef = f32[2,6,1024]{2,1,0:T(8,128)} copy(f32[2,6,1024]{2,0,1:T(2,128)} %param.15) | data formatting | bytes 98304 | tf_op args[2]
  2.1 44.5 %shard_map.127 = f32[3,64,1024]{2,1,0:T(8,128)} custom-call(f32[3,64,1024]{2,1,0:T(8,128)} %state.1, f32[1,1024]{1,0:T(1,128)} %bitcast.3, f32[2,6,1024]{2,1,0:T(8,128)} %copy.14.coef, s32[6,1024]{1,0:T(8,128)} %wet.1, s32[6,1024]{1,0:T(8,128)} %conn.1, s32[2,256]{1,0:T(2,128)} %lists.1, s32[3,1024]{1,0:T(4,128)} %obs_nodes.1, f32[3,1024]{1,0:T(4,128)} %obs_weight.1, ...), custom_call_target="tpu_custom_call" | custom-call | tf_op jit(solution)/shard_map/pallas_call | solution.py:388
  46.6 2.1 %copy.17 = f32[3,64,1024]{2,1,0:T(8,128)} copy(f32[3,64,1024]{2,1,0:T(8,128)} %shard_map.127) | data formatting | bytes 1572864
where the time goes:
time: 49 us; the launch traced here: 48.7 us
  Pallas kernels  44.5 us (91%)
  local copies, waits for them, and re-layouts  3.54 us (7%)
  between operations  0.66 us (1%)
    pallas_call x1, Pallas kernels, local(): pl.pallas_call(functools.partial(kernel, n), out_shape=jax.ShapeDtypeStru...  44.5 us
    unnamed x2, local copies, waits for them, and re-layouts  3.54 us

commit v1 on v0

--- a/solution.py
+++ b/solution.py
@@ -78,31 +78,33 @@
     for b in range(count):
         first = b * width
         panel = blocks[b]
-        rows = [panel[j : j + 1] for j in range(width)]
-        below = blocks[b + 1 :]
-        cols = [[blk[:, first + j : first + j + 1] for blk in below] for j in range(width)]
-        corner = [[panel[j : j + 1, first + i : first + i + 1] for i in range(width)] for j in range(width)]
-        scaled = []
+        full = (width, work.shape[1])
+        rows = [jnp.broadcast_to(panel[j : j + 1], full) for j in range(width)]
+        corner = {
+            (j, i): jnp.broadcast_to(panel[j : j + 1, first + i : first + i + 1], full)
+            for j in range(width) for i in range(j, width)
+        }
+        scaled, scales = [], {}
         for j in range(width):
-            inverse = 1.0 / corner[j][j]
-            unit_row = rows[j] * inverse
-            scaled.append(unit_row)
+            inverse = 1.0 / corner[j, j]
+            scaled.append(rows[j] * inverse)
             for i in range(j + 1, width):
-                factor = corner[j][i]
-                rows[i] = rows[i] - factor * unit_row
-                scale = factor * inverse
-                cols[i] = [ci - cj * scale for ci, cj in zip(cols[i], cols[j])]
+                scales[j, i] = corner[j, i] * inverse
+            for i in range(j + 1, width):
+                rows[i] = rows[i] - scales[j, i] * rows[j]
                 for k in range(i, width):
-                    value = corner[i][k] - scale * corner[j][k]
-                    corner[i][k] = value
-                    corner[k][i] = value
+                    corner[i, k] = corner[i, k] - scales[j, i] * corner[j, k]
         for j in range(width):
-            done.append(rows[j] * lax.rsqrt(corner[j][j]))
-        for n in range(len(below)):
-            total = below[n]
+            done.append((rows[j] * lax.rsqrt(corner[j, j]))[:1])
+        if b + 1 < count:
+            for j in reversed(range(width)):
+                for i in range(j + 1, width):
+                    scaled[j] = scaled[j] - scales[j, i] * scaled[i]
+        for n in range(b + 1, count):
+            total = blocks[n]
             for j in range(width):
-                total = total - cols[j][n] * scaled[j]
-            blocks[b + 1 + n] = total
+                total = total - blocks[n][:, first + j : first + j + 1] * scaled[j]
+            blocks[n] = total
     return jnp.concatenate(done, axis=0)[:, members:]
 
 
@@ -240,7 +242,7 @@
     start(share_copies)
 
     faces = wet[...].astype(F32)
-    east, north = faces * coef[0], faces * coef[1]
+    east, north = faces * coef[:, 0], faces * coef[:, 1]
     totals[0:1] = jnp.sum(east, axis=0, keepdims=True)
     totals[1:2] = jnp.sum(north, axis=0, keepdims=True)
     ids, (east_slots, north_slots) = merge_slots(
@@ -417,7 +419,7 @@
         ],
         compiler_params=pltpu.CompilerParams(collective_id=0, has_side_effects=True, vmem_limit_bytes=56 * 1024 * 1024),
     )(
-        state, depth[None], coef, wet_faces, conn, send_list, obs_nodes, obs_weight, obs_value[None], obs_error[None],
+        state, depth[None], jnp.swapaxes(coef, 0, 1), wet_faces, conn, send_list, obs_nodes, obs_weight, obs_value[None], obs_error[None],
         loc_ids, loc_len, loc_weight,
     )
 

time: 49 us -> 41.5 us (0.85)
  Pallas kernels: 44.5 us -> 38.6 us
  local copies, waits for them, and re-layouts: 3.54 us -> 2.09 us
    pallas_call x1, Pallas kernels: 44.5 us -> 38.6 us  [local(): pl.pallas_call(functools.partial(kernel, n), out_shape=jax.ShapeDtypeStru...]
    unnamed x2 -> x1, local copies, waits for them, and re-layouts: 3.54 us -> 2.09 us
where the time goes in v1:
time: 41.5 us; the launch traced here: 41.3 us
  Pallas kernels  38.6 us (93%)
  local copies, waits for them, and re-layouts  2.09 us (5%)
  between operations  0.66 us (2%)
    pallas_call x1, Pallas kernels, local(): pl.pallas_call(functools.partial(kernel, n), out_shape=jax.ShapeDtypeStru...  38.6 us
    unnamed x1, local copies, waits for them, and re-layouts  2.09 us

profile of v1, /device:TPU:1, one launch (start us, length us, event | category | flops | bytes accessed | tf_op | source)
XLA Modules:
  0.0 41.3 jit_solution(10381244844969656432)
XLA Ops:
  0.7 38.6 %shard_map.127 = f32[3,64,1024]{2,1,0:T(8,128)} custom-call(f32[3,64,1024]{2,1,0:T(8,128)} %state.1, f32[1,1024]{1,0:T(1,128)} %bitcast.5, f32[6,2,1024]{2,1,0:T(2,128)} %bitcast.4, s32[6,1024]{1,0:T(8,128)} %wet.1, s32[6,1024]{1,0:T(8,128)} %conn.1, s32[2,256]{1,0:T(2,128)} %lists.1, s32[3,1024]{1,0:T(4,128)} %obs_nodes.1, f32[3,1024]{1,0:T(4,128)} %obs_weight.1, ...), custom_call_target="tpu_custom_call" | custom-call | tf_op jit(solution)/shard_map/pallas_call | solution.py:390
  39.2 2.1 %copy.16 = f32[3,64,1024]{2,1,0:T(8,128)} copy(f32[3,64,1024]{2,1,0:T(8,128)} %shard_map.127) | data formatting | bytes 1572864
